TPU v7x, 512 devices: a whole 4x4x16 slice. The times are simulated.
512 devices in a mesh: cyc: 16 (over z), tile: 32 (over x, y, core).
Axes of the slice: x: 4, y: 4, z: 16, core: 2. Of those that a mesh axis runs over, the one named last changes fastest.
Arguments:
- weight_change: bfloat16 [16, 80, 80, 1024], P('cyc', None, None, 'tile'), may hold values from -0.1796875 to 0.1796875
- ensemble: bfloat16 [16, 80, 8, 16384], P('cyc', None, None, 'tile'), may hold values from -6 to 6
- stencil_index: int32 [4, 16384], P(None, 'tile'), may hold values from 0 to 39
- stencil_weight: float32 [4, 16384], P(None, 'tile'), may hold values from 0.1 to 1
Outputs:
- smoothed: bfloat16 [16, 80, 8, 16384], P('cyc', None, None, 'tile')
Inputs may be any that keep to these rules, and one draw needn't show every extreme that they name: `stencil_index`: positions 0 to 3 of the extended list are the last columns of the sector before (periodic in longitude), positions 36 and beyond the first columns of the sector after.
All inputs are finite; a program needn't handle non-finite values.
Results may differ from a plain program's by a relative error of at most 0.0085.
Values may be sent and summed in bfloat16 or wider, within the bound.
No kernel may reach another device: no remote copies, remote signals or barrier semaphores. Data moves between devices by JAX's collectives and lax.ppermute only.
A program may use at most 128 MiB of HBM per device.

v0:
```python
import math
import jax
import jax.numpy as jnp
from jax import lax
from jax.sharding import PartitionSpec as P

RIM_COLS = 4


def with_halo(block, sides, width):
    for axis, dim in sides:
        count = lax.axis_size(axis)
        forward = [(i, i + 1) for i in range(count - 1)]
        forward.append((count - 1, 0))
        backward = [(target, source) for source, target in forward]
        low = lax.ppermute(
            lax.slice_in_dim(block, block.shape[dim] - width, None, axis=dim), axis, forward
        )
        high = lax.ppermute(lax.slice_in_dim(block, 0, width, axis=dim), axis, backward)
        block = jnp.concatenate([low, block, high], axis=dim)
    return block


def combine(earlier, later):
    return jnp.einsum(
        "ijg,jkg->ikg",
        later,
        earlier,
        precision=lax.Precision.HIGHEST,
        preferred_element_type=jnp.float32,
    )


def suffix_of(raw, eye):
    mats = raw.astype(jnp.float32) + eye
    unity = jnp.broadcast_to(eye, mats.shape)
    every = lax.all_gather(raw[None], "cyc", axis=0, tiled=True)
    count = every.shape[0]
    mine = lax.axis_index("cyc")

    def step(number, carry):
        later_cycle = count - 1 - number
        weight = (
            lax.dynamic_index_in_dim(every, later_cycle, 0, keepdims=False).astype(jnp.float32)
            + eye
        )
        product = combine(carry, weight)
        return jnp.where(later_cycle > mine, product, carry)

    return lax.fori_loop(0, count, step, unity)


def on_device(weight_change, ensemble, stencil_index, stencil_weight):
    members = weight_change.shape[1]
    eye = jnp.eye(members, dtype=jnp.float32)[:, :, None]
    suffix = suffix_of(weight_change[0], eye)
    extended = with_halo(suffix, (("tile", 2),), RIM_COLS)
    width = extended.shape[2]
    flat = extended.reshape(members * members, width)
    shares = stencil_weight / jnp.sum(stencil_weight, axis=0, keepdims=True)
    states = ensemble[0]
    points = states.shape[2]
    block = math.gcd(points, 256)
    blocks = points // block
    slots = jnp.arange(width)[:, None]

    def one_block(number, output):
        begin = number * block
        index = lax.dynamic_slice_in_dim(stencil_index, begin, block, 1)
        weights = lax.dynamic_slice_in_dim(shares, begin, block, 1)
        table = jnp.zeros((width, block), jnp.float32)
        for corner in range(4):
            table = table + jnp.where(
                index[corner][None, :] == slots, weights[corner][None, :], 0.0
            )
        interp = jnp.dot(
            flat, table, precision=lax.Precision.HIGHEST, preferred_element_type=jnp.float32
        )
        interp = interp.reshape(members, members, block).astype(jnp.bfloat16)
        piece = lax.dynamic_slice_in_dim(states, begin, block, 2)
        mixed = jnp.einsum(
            "nvf,nmf->mvf", piece, interp, preferred_element_type=jnp.float32
        ).astype(jnp.bfloat16)
        return lax.dynamic_update_slice_in_dim(output, mixed, begin, 2)

    result = lax.fori_loop(0, blocks, one_block, jnp.zeros_like(states))
    return result[None]


def solution(mesh):
    placed = (
        P("cyc", None, None, "tile"),
        P("cyc", None, None, "tile"),
        P(None, "tile"),
        P(None, "tile"),
    )
    return jax.shard_map(
        on_device,
        mesh=mesh,
        in_specs=placed,
        out_specs=P("cyc", None, None, "tile"),
        check_vma=False,
    )
```

profile of v0, /device:TPU:31, one launch (start us, length us, event | category | flops | bytes accessed | tf_op | source)
XLA Modules:
  0.0 262.1 jit_solution(1129115053120165722)
XLA Ops:
  8.0 132.4 %all-gather.2.cloned.1.call-done = bf16[16,80,80,32]{2,3,1,0:T(8,128)(2,1)} async-done(((bf16[1,80,80,32]{2,3,1,0:T(8,128)(2,1)}), bf16[16,80,80,32]{2,3,1,0:T(8,128)(2,1)}) %all-gather.2.cloned.1.call-update) | async-done | bytes 6553616 | tf_op jit(solution)/shard_map/all_gather | solution.py:37
  140.5 48.1 %while.31 = (s32[]{:T(128)}, f32[80,80,32]{1,0,2:T(8,128)S(1)}, s32[]{:T(128)}, bf16[16,80,80,32]{2,3,1,0:T(8,128)(2,1)}, s32[]{:T(128)}, /*index=5*/s32[]{:T(128)}, s32[]{:T(128)}, s32[]{:T(128)}) while((s32[]{:T(128)}, f32[80,80,32]{1,0,2:T(8,128)S(1)}, s32[]{:T(128)}, bf16[16,80,80,32]{2,3,1,0:T(8,128)(2,1)}, s32[]{:T(128)}, ...), condition=%wide.region_2.3_spmd.clone, body=%wide.region_1.2_spmd.clone.sunk | while | flops 197235200 | bytes 4556945 | solution.py:50
  140.5 1.2 constant_dynamic-slice_fusion.6
  141.8 1.7 fusion.41
  143.5 1.1 constant_dynamic-slice_fusion.6
  144.8 1.7 fusion.41
  146.6 1.1 constant_dynamic-slice_fusion.6
  147.8 1.7 fusion.41
  149.6 1.1 constant_dynamic-slice_fusion.6
  150.8 1.7 fusion.41
  152.6 1.1 constant_dynamic-slice_fusion.6
  153.8 1.7 fusion.41
  155.6 1.1 constant_dynamic-slice_fusion.6
  156.8 1.7 fusion.41
  158.6 1.1 constant_dynamic-slice_fusion.6
  159.8 1.7 fusion.41
  161.6 1.1 constant_dynamic-slice_fusion.6
  162.8 1.7 fusion.41
  164.6 1.1 constant_dynamic-slice_fusion.6
  165.8 1.7 fusion.41
  167.6 1.1 constant_dynamic-slice_fusion.6
  168.8 1.7 fusion.41
  170.6 1.1 constant_dynamic-slice_fusion.6
  171.8 1.7 fusion.41
  173.6 1.1 constant_dynamic-slice_fusion.6
  174.8 1.7 fusion.41
  176.6 1.1 constant_dynamic-slice_fusion.6
  177.8 1.7 fusion.41
  179.6 1.1 constant_dynamic-slice_fusion.6
  180.8 1.7 fusion.41
  182.6 1.1 constant_dynamic-slice_fusion.6
  183.8 1.7 fusion.41
  185.6 1.1 constant_dynamic-slice_fusion.6
  186.8 1.7 fusion.41
  188.6 2.8 %collective-permute-start = (f32[80,80,4]{1,0,2:T(8,128)S(1)}, f32[80,80,4]{1,0,2:T(8,128)S(1)}, u32[]{:S(2)}, u32[]{:S(2)}) collective-permute-start(f32[80,80,4]{1,0,2:T(8,128)S(1)} %get-tuple-element.348), channel_id=1, source_target_pairs={{0,1},{1,2},{2,3},{3,4},{4,5},{5,6},{6,7},{7,8},{8,9},{9,10},{10,1... | collective-permute-start | bytes 307208 | tf_op jit(solution)/shard_map/ppermute | solution.py:16
  191.5 1.9 collective-permute-start.1
  193.4 1.7 copy.19
  195.2 6.2 %collective-permute-done.1 = f32[80,80,4]{1,0,2:T(8,128)S(1)} collective-permute-done((f32[80,80,4]{1,0,2:T(8,128)S(1)}, f32[80,80,4]{1,0,2:T(8,128)S(1)}, u32[]{:S(2)}, u32[]{:S(2)}) %collective-permute-start.1) | collective-permute-done | bytes 102432 | tf_op jit(solution)/shard_map/ppermute | solution.py:19
  201.5 2.4 copy.18
  204.8 50.4 %while.32 = (s32[]{:T(128)}, bf16[80,8,512]{2,1,0:T(8,128)(2,1)}, s32[4,512]{1,0:T(4,128)S(1)}, f32[4,512]{1,0:T(4,128)S(1)}, f32[6400,40]{1,0:T(8,128)}, /*inde...) while((s32[]{:T(128)}, bf16[80,8,512]{2,1,0:T(8,128)(2,1)}, ...), condition=%wide.region_4.5_spmd.clone.clone, body=%wide.region_3.4_spmd.clone.clone.sunk | while | flops 814561280 | bytes 30736716 | solution.py:86
  205.0 8.2 %fusion.46 = bf16[6400,256]{0,1:T(8,128)(2,1)S(1)} fusion(f32[6400,40]{1,0:T(8,128)} %get-tuple-element.482, f32[256]{0:T(256)S(1)} %bitcast.71, s32[256]{0:T(256)S(1)} %bitcast.75, f32[256]{0:T(256)S(1)} %bitcast.69, s32[256]{0:T(256)S(1)} %bitcast.73, f32[256]{0:T(256)S(1)} %bitcast.70, s32[256]{0:T(256)S(1)} %bitcast.74, f32[256]{0:T(256)S(1)} %bitcast.68, ...), kind=kOutput, calls=%fused_computation.11.clone.1 | convolution fusion | flops 788183040 | bytes 4308992 | tf_op jit(solution)/shard_map/while/body/eval_jaxpr/dot_general | solution.py:76
  213.1 3.5 %copy.33 = bf16[6400,256]{1,0:T(8,128)(2,1)} copy(bf16[6400,256]{0,1:T(8,128)(2,1)S(1)} %fusion.46) | data formatting | bytes 6553600 | tf_op jit(solution)/shard_map/while/body/eval_jaxpr/convert_element_type | solution.py:79
  216.6 8.0 %copy.34 = bf16[80,80,256]{1,0,2:T(8,128)(2,1)} copy(bf16[80,80,256]{2,1,0:T(8,128)(2,1)} %bitcast.65) | data formatting | bytes 6553600 | tf_op jit(solution)/shard_map/while/body/eval_jaxpr/convert_element_type | solution.py:79
  224.6 4.0 %fusion.47 = bf16[80,8,256]{0,1,2:T(8,128)(2,1)S(1)} fusion(bf16[80,80,256]{1,0,2:T(8,128)(2,1)} %copy.34, bf16[80,8,512]{0,1,2:T(8,128)(2,1)S(1)} %copy-done, s32[]{:T(128)S(6)} %select_n.118), kind=kOutput, calls=%fused_computation.13.clone.1 | convolution fusion | flops 26378240 | bytes 4128772 | tf_op jit(solution)/shard_map/while/body/eval_jaxpr/nvf,nmf->mvf/dot_general | solution.py:81
  230.2 8.2 %fusion.46 = bf16[6400,256]{0,1:T(8,128)(2,1)S(1)} fusion(f32[6400,40]{1,0:T(8,128)} %get-tuple-element.482, f32[256]{0:T(256)S(1)} %bitcast.71, s32[256]{0:T(256)S(1)} %bitcast.75, f32[256]{0:T(256)S(1)} %bitcast.69, s32[256]{0:T(256)S(1)} %bitcast.73, f32[256]{0:T(256)S(1)} %bitcast.70, s32[256]{0:T(256)S(1)} %bitcast.74, f32[256]{0:T(256)S(1)} %bitcast.68, ...), kind=kOutput, calls=%fused_computation.11.clone.1 | convolution fusion | flops 788183040 | bytes 4308992 | tf_op jit(solution)/shard_map/while/body/eval_jaxpr/dot_general | solution.py:76
  238.4 3.5 %copy.33 = bf16[6400,256]{1,0:T(8,128)(2,1)} copy(bf16[6400,256]{0,1:T(8,128)(2,1)S(1)} %fusion.46) | data formatting | bytes 6553600 | tf_op jit(solution)/shard_map/while/body/eval_jaxpr/convert_element_type | solution.py:79
  241.8 8.0 %copy.34 = bf16[80,80,256]{1,0,2:T(8,128)(2,1)} copy(bf16[80,80,256]{2,1,0:T(8,128)(2,1)} %bitcast.65) | data formatting | bytes 6553600 | tf_op jit(solution)/shard_map/while/body/eval_jaxpr/convert_element_type | solution.py:79
  249.8 4.0 %fusion.47 = bf16[80,8,256]{0,1,2:T(8,128)(2,1)S(1)} fusion(bf16[80,80,256]{1,0,2:T(8,128)(2,1)} %copy.34, bf16[80,8,512]{0,1,2:T(8,128)(2,1)S(1)} %copy-done, s32[]{:T(128)S(6)} %select_n.118), kind=kOutput, calls=%fused_computation.13.clone.1 | convolution fusion | flops 26378240 | bytes 4128772 | tf_op jit(solution)/shard_map/while/body/eval_jaxpr/nvf,nmf->mvf/dot_general | solution.py:81
  (68 shorter events, 7.1 us)
Async XLA Ops:
  6.5 133.8 %all-gather.2.cloned.1.call-start = ((), (), s32[]{:S(2)}) async-start(), calls=%async_computation | async-start | bytes 11141120 | tf_op jit(solution)/shard_map/all_gather | solution.py:37
  140.4 52.9 %copy-start.5 = (f32[4,512]{1,0:T(4,128)S(1)}, f32[4,512]{1,0:T(4,128)}, u32[]{:S(2)}) copy-start(f32[4,512]{1,0:T(4,128)} %param.11) | copy-start | bytes 24580
  140.5 53.0 %copy-start.1 = (bf16[1,80,8,512]{3,2,1,0:T(8,128)(2,1)S(1)}, bf16[1,80,8,512]{3,2,1,0:T(8,128)(2,1)}, u32[]{:S(2)}) copy-start(bf16[1,80,8,512]{3,2,1,0:T(8,128)(2,1)} %param.9) | copy-start | bytes 1966084
  188.6 6.6 %collective-permute-start = (f32[80,80,4]{1,0,2:T(8,128)S(1)}, f32[80,80,4]{1,0,2:T(8,128)S(1)}, u32[]{:S(2)}, u32[]{:S(2)}) collective-permute-start(f32[80,80,4]{1,0,2:T(8,128)S(1)} %get-tuple-element.348), channel_id=1, source_target_pairs={{0,1},{1,2},{2,3},{3,4},{4,5},{5,6},{6,7},{7,8},{8,9},{9,10},{10,1... | collective-permute-start | bytes 307208 | tf_op jit(solution)/shard_map/ppermute | solution.py:16
  191.5 10.0 %collective-permute-start.1 = (f32[80,80,4]{1,0,2:T(8,128)S(1)}, f32[80,80,4]{1,0,2:T(8,128)S(1)}, u32[]{:S(2)}, u32[]{:S(2)}) collective-permute-start(f32[80,80,4]{1,0,2:T(8,128)S(1)} %get-tuple-element.349), channel_id=1, source_target_pairs={{1,0},{2,1},{3,2},{4,3},{5,4},{6,5},{7,6},{8,7},{9,8},{10,9},{11,1... | collective-permute-start | bytes 307208 | tf_op jit(solution)/shard_map/ppermute | solution.py:19
  201.5 3.3 %copy-start.4 = (s32[4,512]{1,0:T(4,128)S(1)}, s32[4,512]{1,0:T(4,128)}, u32[]{:S(2)}) copy-start(s32[4,512]{1,0:T(4,128)} %param.10) | copy-start | bytes 24580
  216.6 8.0 %copy-start = (bf16[80,8,512]{0,1,2:T(8,128)(2,1)S(1)}, bf16[80,8,512]{0,1,2:T(8,128)(2,1)}, u32[]{:S(2)}) copy-start(bf16[80,8,512]{0,1,2:T(8,128)(2,1)} %get-tuple-element.483) | copy-start | bytes 1966084 | tf_op jit(solution)/shard_map/while
  224.6 4.5 %copy-start.2 = (bf16[80,8,512]{2,1,0:T(8,128)(2,1)S(1)}, bf16[80,8,512]{2,1,0:T(8,128)(2,1)}, u32[]{:S(2)}) copy-start(bf16[80,8,512]{2,1,0:T(8,128)(2,1)} %get-tuple-element.466) | copy-start | bytes 1966084 | tf_op jit(solution)/shard_map/while
  229.2 0.8 copy-start.3
  241.8 8.0 %copy-start = (bf16[80,8,512]{0,1,2:T(8,128)(2,1)S(1)}, bf16[80,8,512]{0,1,2:T(8,128)(2,1)}, u32[]{:S(2)}) copy-start(bf16[80,8,512]{0,1,2:T(8,128)(2,1)} %get-tuple-element.483) | copy-start | bytes 1966084 | tf_op jit(solution)/shard_map/while
  249.8 4.5 %copy-start.2 = (bf16[80,8,512]{2,1,0:T(8,128)(2,1)S(1)}, bf16[80,8,512]{2,1,0:T(8,128)(2,1)}, u32[]{:S(2)}) copy-start(bf16[80,8,512]{2,1,0:T(8,128)(2,1)} %get-tuple-element.466) | copy-start | bytes 1966084 | tf_op jit(solution)/shard_map/while
  254.4 0.8 copy-start.3
Sparse Core Ops, SparseCore 0:
  9.4 130.8 all-gather.1
where the time goes:
time: 263 us; the launch traced here: 262 us
  waiting for transfers between devices  139 us (53%)
  matrix products  52 us (20%)
  local copies, waits for them, and re-layouts  50.7 us (19%)
  between operations  13.5 us (5%)
  starting transfers between devices  4.75 us (2%)
    all_gather x1, waiting for transfers between devices, suffix_of(): every = lax.all_gather(raw[None], 'cyc', axis=0, tiled=True)  132 us
    dot_general x16, matrix products, combine(): jnp.einsum('ijg,jkg->ikg', later, earlier, precision=lax.Precision.HIGHES...  27.6 us
    convert_element_type x4, local copies, waits for them, and re-layouts, one_block(): interp = interp.reshape(members, members, block).astype(jnp.bfloat16)  22.9 us
    dynamic_slice x16, local copies, waits for them, and re-layouts, step(): lax.dynamic_index_in_dim(every, later_cycle, 0, keepdims=False)  18.2 us
    dot_general x2, matrix products, one_block(): jnp.dot(flat, table, precision=lax.Precision.HIGHEST, preferred_element_t...  16.4 us
    dot_general x2, matrix products, one_block(): jnp.einsum('nvf,nmf->mvf', piece, interp, preferred_element_type=jnp.floa...  8.02 us
    ppermute x1, waiting for transfers between devices, with_halo(): lax.ppermute(lax.slice_in_dim(block, 0, width, axis=dim), axis, backward)  6.25 us
  transfers between devices with their start and end apart: 3, of which 2 were waited for; matrix products, arithmetic and copies ran while one was open for 1% of the time, Pallas kernels for 0%

commit v1 on v0

--- a/solution.py
+++ b/solution.py
@@ -34,7 +34,8 @@
 def suffix_of(raw, eye):
     mats = raw.astype(jnp.float32) + eye
     unity = jnp.broadcast_to(eye, mats.shape)
-    every = lax.all_gather(raw[None], "cyc", axis=0, tiled=True)
+    copies = jnp.concatenate([raw[None]] * lax.axis_size("cyc"), axis=0)
+    every = lax.all_to_all(copies, "cyc", 0, 0, tiled=True)
     count = every.shape[0]
     mine = lax.axis_index("cyc")
 

time: 263 us -> 588 us (2.24)
  the two profiles are of different devices: /device:TPU:31 before, /device:TPU:63 now
where the time goes in v1:
time: 588 us; the launch traced here: 587 us
  waiting for transfers between devices  459 us (78%)
  matrix products  67.4 us (11%)
  local copies, waits for them, and re-layouts  39.7 us (7%)
  starting transfers between devices  20 us (3%)
    all_to_all x1, waiting for transfers between devices, suffix_of(): every = lax.all_to_all(copies, 'cyc', 0, 0, tiled=True)  453 us
    dot_general x16, matrix products, combine(): jnp.einsum('ijg,jkg->ikg', later, earlier, precision=lax.Precision.HIGHES...  43 us
    convert_element_type x4, local copies, waits for them, and re-layouts, one_block(): interp = interp.reshape(members, members, block).astype(jnp.bfloat16)  23 us
    dot_general x2, matrix products, one_block(): jnp.dot(flat, table, precision=lax.Precision.HIGHEST, preferred_element_t...  16.4 us
    all_to_all x1, starting transfers between devices, suffix_of(): every = lax.all_to_all(copies, 'cyc', 0, 0, tiled=True)  14.8 us
  transfers between devices with their start and end apart: 3, of which 2 were waited for; matrix products, arithmetic and copies ran while one was open for 0% of the time, Pallas kernels for 0%

profile of v1, /device:TPU:63, one launch (start us, length us, event | category | flops | bytes accessed | tf_op | source)
XLA Modules:
  0.0 587.0 jit_solution(16282596285320945557)
XLA Ops:
  0.0 1.3 copy.11
  1.3 5.8 concatenate.6
  7.2 14.8 %all-to-all-start = ((bf16[16,80,80,32]{2,1,3,0:T(8,128)(2,1)}), bf16[16,80,80,32]{2,1,3,0:T(8,128)(2,1)}, u32[]{:S(2)}, u32[]{:S(2)}) async-start(bf16[16,80,80,32]{2,1,3,0:T(8,128)(2,1)} %concatenate.6), calls=%async_computation | async-start | bytes 20971520 | tf_op jit(solution)/shard_map/all_to_all | solution.py:38
  22.0 452.7 %all-to-all-done = bf16[16,80,80,32]{2,1,3,0:T(8,128)(2,1)} async-done(((bf16[16,80,80,32]{2,1,3,0:T(8,128)(2,1)}), bf16[16,80,80,32]{2,1,3,0:T(8,128)(2,1)}, u32[]{:S(2)}, u32[]{:S(2)}) %all-to-all-start) | async-done | bytes 6553632 | tf_op jit(solution)/shard_map/all_to_all | solution.py:38
  474.8 45.3 %while.31 = (s32[]{:T(128)}, f32[80,80,32]{1,0,2:T(8,128)S(1)}, s32[]{:T(128)}, bf16[16,80,80,32]{2,1,3,0:T(8,128)(2,1)}, s32[]{:T(128)}, /*index=5*/s32[]{:T(128)}, s32[]{:T(128)}, s32[]{:T(128)}) while((s32[]{:T(128)}, f32[80,80,32]{1,0,2:T(8,128)S(1)}, s32[]{:T(128)}, bf16[16,80,80,32]{2,1,3,0:T(8,128)(2,1)}, s32[]{:T(128)}, ...), condition=%wide.region_2.3_spmd.clone, body=%wide.region_1.2_spmd.clone.sunk | while | flops 197235200 | bytes 5801105 | solution.py:51
  474.9 2.7 fusion.44
  477.7 0.1 copy.37
  477.8 2.7 fusion.44
  480.5 0.1 copy.37
  480.6 2.7 fusion.44
  483.3 0.1 copy.37
  483.5 2.7 fusion.44
  486.3 2.7 fusion.44
  489.0 0.1 copy.37
  489.1 2.7 fusion.44
  491.8 0.1 copy.37
  491.9 2.7 fusion.44
  494.7 0.1 copy.37
  494.8 2.7 fusion.44
  497.5 0.1 copy.37
  497.6 2.7 fusion.44
  500.4 2.7 fusion.44
  503.3 2.7 fusion.44
  506.1 2.7 fusion.44
  508.9 2.7 fusion.44
  511.7 2.7 fusion.44
  514.6 2.7 fusion.44
  517.4 2.7 fusion.44
  520.1 3.0 collective-permute-start
  523.2 2.2 collective-permute-start.1
  525.4 1.7 copy.13
  527.1 6.0 %collective-permute-done.1 = f32[80,80,4]{1,0,2:T(8,128)S(1)} collective-permute-done((f32[80,80,4]{1,0,2:T(8,128)S(1)}, f32[80,80,4]{1,0,2:T(8,128)S(1)}, u32[]{:S(2)}, u32[]{:S(2)}) %collective-permute-start.1) | collective-permute-done | bytes 102432 | tf_op jit(solution)/shard_map/ppermute | solution.py:19
  533.1 0.1 pad_maximum_fusion
  533.3 2.4 copy.12
  535.6 0.9 broadcast_in_dim.96.clone
  536.5 50.5 %while.32 = (s32[]{:T(128)}, bf16[80,8,512]{2,1,0:T(8,128)(2,1)}, s32[4,512]{1,0:T(4,128)S(1)}, f32[4,512]{1,0:T(4,128)S(1)}, f32[6400,40]{1,0:T(8,128)}, /*inde...) while((s32[]{:T(128)}, bf16[80,8,512]{2,1,0:T(8,128)(2,1)}, ...), condition=%wide.region_4.5_spmd.clone.clone, body=%wide.region_3.4_spmd.clone.clone.sunk | while | flops 814561280 | bytes 30736716 | solution.py:87
  536.7 8.2 %fusion.49 = bf16[6400,256]{0,1:T(8,128)(2,1)S(1)} fusion(f32[6400,40]{1,0:T(8,128)} %get-tuple-element.478, f32[256]{0:T(256)S(1)} %bitcast.73, s32[256]{0:T(256)S(1)} %bitcast.77, f32[256]{0:T(256)S(1)} %bitcast.71, s32[256]{0:T(256)S(1)} %bitcast.75, f32[256]{0:T(256)S(1)} %bitcast.72, s32[256]{0:T(256)S(1)} %bitcast.76, f32[256]{0:T(256)S(1)} %bitcast.70, ...), kind=kOutput, calls=%fused_computation.12.clone.1 | convolution fusion | flops 788183040 | bytes 4308992 | tf_op jit(solution)/shard_map/while/body/eval_jaxpr/dot_general | solution.py:77
  544.9 3.5 copy.20
  548.3 8.0 %copy.21 = bf16[80,80,256]{1,0,2:T(8,128)(2,1)} copy(bf16[80,80,256]{2,1,0:T(8,128)(2,1)} %bitcast.66) | data formatting | bytes 6553600 | tf_op jit(solution)/shard_map/while/body/eval_jaxpr/convert_element_type | solution.py:80
  556.4 4.0 fusion.50
  560.4 0.5 copy.22
  560.9 0.8 copy-done.3
  561.9 8.2 %fusion.49 = bf16[6400,256]{0,1:T(8,128)(2,1)S(1)} fusion(f32[6400,40]{1,0:T(8,128)} %get-tuple-element.478, f32[256]{0:T(256)S(1)} %bitcast.73, s32[256]{0:T(256)S(1)} %bitcast.77, f32[256]{0:T(256)S(1)} %bitcast.71, s32[256]{0:T(256)S(1)} %bitcast.75, f32[256]{0:T(256)S(1)} %bitcast.72, s32[256]{0:T(256)S(1)} %bitcast.76, f32[256]{0:T(256)S(1)} %bitcast.70, ...), kind=kOutput, calls=%fused_computation.12.clone.1 | convolution fusion | flops 788183040 | bytes 4308992 | tf_op jit(solution)/shard_map/while/body/eval_jaxpr/dot_general | solution.py:77
  570.1 3.5 copy.20
  573.6 8.0 %copy.21 = bf16[80,80,256]{1,0,2:T(8,128)(2,1)} copy(bf16[80,80,256]{2,1,0:T(8,128)(2,1)} %bitcast.66) | data formatting | bytes 6553600 | tf_op jit(solution)/shard_map/while/body/eval_jaxpr/convert_element_type | solution.py:80
  581.6 4.0 fusion.50
  585.6 0.5 copy.22
  586.2 0.8 copy-done.3
  (53 shorter events, 1.5 us)
Async XLA Ops:
  7.2 14.8 %copy-start.5 = (f32[4,512]{1,0:T(4,128)S(1)}, f32[4,512]{1,0:T(4,128)}, u32[]{:S(2)}) copy-start(f32[4,512]{1,0:T(4,128)} %param.11) | copy-start | bytes 24580
  7.2 467.5 %all-to-all-start = ((bf16[16,80,80,32]{2,1,3,0:T(8,128)(2,1)}), bf16[16,80,80,32]{2,1,3,0:T(8,128)(2,1)}, u32[]{:S(2)}, u32[]{:S(2)}) async-start(bf16[16,80,80,32]{2,1,3,0:T(8,128)(2,1)} %concatenate.6), calls=%async_computation | async-start | bytes 20971520 | tf_op jit(solution)/shard_map/all_to_all | solution.py:38
  474.8 50.6 %copy-start.1 = (bf16[1,80,8,512]{3,2,1,0:T(8,128)(2,1)S(1)}, bf16[1,80,8,512]{3,2,1,0:T(8,128)(2,1)}, u32[]{:S(2)}) copy-start(bf16[1,80,8,512]{3,2,1,0:T(8,128)(2,1)} %param.9) | copy-start | bytes 1966084
  520.1 7.0 %collective-permute-start = (f32[80,80,4]{1,0,2:T(8,128)S(1)}, f32[80,80,4]{1,0,2:T(8,128)S(1)}, u32[]{:S(2)}, u32[]{:S(2)}) collective-permute-start(f32[80,80,4]{1,0,2:T(8,128)S(1)} %get-tuple-element.344), channel_id=1, source_target_pairs={{0,1},{1,2},{2,3},{3,4},{4,5},{5,6},{6,7},{7,8},{8,9},{9,10},{10,1... | collective-permute-start | bytes 307208 | tf_op jit(solution)/shard_map/ppermute | solution.py:16
  523.2 10.0 %collective-permute-start.1 = (f32[80,80,4]{1,0,2:T(8,128)S(1)}, f32[80,80,4]{1,0,2:T(8,128)S(1)}, u32[]{:S(2)}, u32[]{:S(2)}) collective-permute-start(f32[80,80,4]{1,0,2:T(8,128)S(1)} %get-tuple-element.345), channel_id=1, source_target_pairs={{1,0},{2,1},{3,2},{4,3},{5,4},{6,5},{7,6},{8,7},{9,8},{10,9},{11,1... | collective-permute-start | bytes 307208 | tf_op jit(solution)/shard_map/ppermute | solution.py:19
  533.3 3.3 copy-start.4
  548.3 8.1 %copy-start = (bf16[80,8,512]{0,1,2:T(8,128)(2,1)S(1)}, bf16[80,8,512]{0,1,2:T(8,128)(2,1)}, u32[]{:S(2)}) copy-start(bf16[80,8,512]{0,1,2:T(8,128)(2,1)} %get-tuple-element.479) | copy-start | bytes 1966084 | tf_op jit(solution)/shard_map/while
  556.4 4.5 copy-start.2
  560.9 0.8 copy-start.3
  573.6 8.1 %copy-start = (bf16[80,8,512]{0,1,2:T(8,128)(2,1)S(1)}, bf16[80,8,512]{0,1,2:T(8,128)(2,1)}, u32[]{:S(2)}) copy-start(bf16[80,8,512]{0,1,2:T(8,128)(2,1)} %get-tuple-element.479) | copy-start | bytes 1966084 | tf_op jit(solution)/shard_map/while
  581.6 4.5 copy-start.2
  586.2 0.8 copy-start.3
